TPU v7x, 256 devices: a 4x2x16 block of a 4x16x16 slice. The times are simulated.
256 devices in a mesh: win: 2 (over y), row: 128 (over x, z, core).
Axes of the slice: x: 4, y: 2, z: 16, core: 2. Of those that a mesh axis runs over, the one named last changes fastest.
The devices are a block of a 4x16x16 slice.
Arguments:
- spectra: bfloat16 [256, 2, 32768], P(('win', 'row')), parts along dimension 0, may hold values from -6 to 6
- pair_mask: int32 [128, 128], P('row'), may hold values from 0 to 1, as said below
- available: int32 [256], P('win'), parts along dimension 0, may hold values 0 or 1
Outputs:
- correlations: float32 [256, 128, 8192], P(('win', 'row')), parts along dimension 0
There are 2 independent parts, one for each index of `win`. A program takes and returns all parts, laid end to end along the dimension named above; an argument that names none is the same for every part. Nothing has to cross between parts.
Inputs may be any that keep to these rules, and one draw needn't show every extreme that they name: pair_mask[i, j] is 0 wherever j <= i.
All inputs are finite; a program needn't handle non-finite values.
Results may differ from a plain program's by a relative error of at most 0.0003.
Values may be sent and summed in bfloat16 or wider, within the bound.
No kernel may reach another device: no remote copies, remote signals or barrier semaphores. Data moves between devices by JAX's collectives and lax.ppermute only.
A program may use at most 128 MiB of HBM per device.

v0:
```python
import math
import jax
import jax.numpy as jnp
from jax import lax
from jax.sharding import PartitionSpec as P

LAGS = 8192
full_turn = 2.0 * math.pi


def build_tables(freq, lags):
    nfft = 2 * freq
    inner = min(128, lags // 2)
    column = nfft // inner
    depth = freq // column
    outer = lags // inner
    centre = lags // 2
    t_inner = jnp.arange(inner, dtype=jnp.int32)
    k_depth = jnp.arange(depth, dtype=jnp.int32)
    k_column = jnp.arange(column, dtype=jnp.int32)
    t_outer = jnp.arange(outer, dtype=jnp.int32)
    first = full_turn * (t_inner[:, None] * k_depth[None, :] % inner).astype(jnp.float32) / inner
    cos_first = jnp.cos(first)
    sin_first = jnp.sin(first)
    section_one = jnp.concatenate(
        [
            jnp.concatenate([cos_first, -sin_first], axis=1),
            jnp.concatenate([sin_first, cos_first], axis=1),
        ],
        axis=0,
    )
    twist = (
        full_turn
        * jnp.mod(k_column[None, :] * (t_inner[:, None] - centre), nfft).astype(jnp.float32)
        / nfft
    )
    second = (
        full_turn * (t_outer[:, None] * k_column[None, :] % column).astype(jnp.float32) / column
    )
    section_two = jnp.stack([jnp.cos(second), -jnp.sin(second)], axis=1)
    return (section_one, jnp.cos(twist), jnp.sin(twist), section_two)


def pair_block(own_wide, part, signs, tables):
    section_one, twist_cos, twist_sin, section_two = tables
    count = own_wide.shape[0]
    width = part.shape[0]
    freq = part.shape[2]
    inner = twist_cos.shape[0]
    column = twist_cos.shape[1]
    outer = section_two.shape[0]
    depth = freq // column
    other = part.astype(jnp.float32)
    real_part = (
        own_wide[:, None, 0, :] * other[None, :, 0, :]
        + own_wide[:, None, 1, :] * other[None, :, 1, :]
    )
    imag_part = (
        own_wide[:, None, 0, :] * other[None, :, 1, :]
        - own_wide[:, None, 1, :] * other[None, :, 0, :]
    ) * signs[:, :, None]
    cross = jnp.stack([real_part, imag_part], axis=2).reshape(count * width, 2 * depth, column)
    mixed = jnp.einsum("uv,pvk->puk", section_one, cross, precision=lax.Precision.HIGH)
    mixed = mixed.reshape(count * width, 2, inner, column)
    turned_real = mixed[:, 0] * twist_cos - mixed[:, 1] * twist_sin
    turned_imag = mixed[:, 0] * twist_sin + mixed[:, 1] * twist_cos
    turned = jnp.stack([turned_real, turned_imag], axis=1)
    summed = jnp.einsum("tck,pcuk->ptu", section_two, turned, precision=lax.Precision.HIGH)
    summed = summed.reshape(count, width, outer * inner)
    return (2.0 * summed - real_part[:, :, :1]) * (1.0 / math.sqrt(8.0 * freq))


def correlate(own, others, signs, tables):
    own_wide = own.astype(jnp.float32)
    count = own.shape[0]
    total = others.shape[0]
    width = math.gcd(total, max(1, 8 // count))
    groups = total // width
    pieces = others.reshape(groups, width, 2, others.shape[2])
    sign_pieces = jnp.transpose(signs.reshape(count, groups, width), (1, 0, 2))

    def one_group(item):
        return pair_block(own_wide, item[0], item[1], tables)

    results = lax.map(one_group, (pieces, sign_pieces))
    return jnp.transpose(results, (1, 0, 2, 3)).reshape(count, total, results.shape[3])


def per_device(spectra, pair_mask, available):
    count = spectra.shape[0]
    freq = spectra.shape[2]
    tables = build_tables(freq, LAGS)
    first_station = lax.axis_index("row") * count
    own_flags = lax.dynamic_slice_in_dim(available, first_station, count, 0).astype(jnp.float32)
    weight = (
        pair_mask.astype(jnp.float32) * own_flags[:, None] * available.astype(jnp.float32)[None, :]
    )
    piece = lax.all_gather(spectra, "row", axis=0, tiled=True)
    corr = correlate(spectra, piece, jnp.ones((count, piece.shape[0]), jnp.float32), tables)
    return corr * weight[:, :, None]


def solution(mesh):
    return jax.shard_map(
        per_device,
        mesh=mesh,
        in_specs=(P(("win", "row"), None, None), P("row", None), P("win")),
        out_specs=P(("win", "row"), None, None),
        check_vma=False,
    )
```

profile of v0, /device:TPU:33, one launch (start us, length us, event | category | flops | bytes accessed | tf_op | source)
XLA Modules:
  0.0 506.9 jit_solution(1056133077329128225)
XLA Ops:
  12.1 166.8 %all-gather.2.cloned.1.call-done = bf16[128,2,32768]{2,1,0:T(2,128)(2,1)} async-done(((bf16[1,2,32768]{2,1,0:T(2,128)(2,1)}), bf16[128,2,32768]{2,1,0:T(2,128)(2,1)}) %all-gather.2.cloned.1.call-update) | async-done | bytes 16777232 | tf_op jit(solution)/shard_map/all_gather | solution.py:98
  178.9 316.4 %while.13 = (s32[]{:T(128)}, f32[16,1,8,8192]{3,2,1,0:T(8,128)}, f32[1,2,32768]{2,1,0:T(2,128)S(1)}, bf16[16,8,2,32768]{3,2,1,0:T(2,128)(2,1)}, f32[256,128]{1,0...) while((s32[]{:T(128)}, f32[16,1,8,8192]{3,2,1,0:T(8,128)}, ...), condition=%wide.region_1.2_spmd.clone.clone.clone, body=%wide.region_0.1_spmd.clone.clone.clone.sunk | while | flops 1215889408 | bytes 57017112 | solution.py:85
  184.3 2.9 copy.24
  187.3 4.0 reshape.466
  204.1 2.9 copy.24
  207.0 4.0 reshape.466
  223.9 2.9 copy.24
  226.8 4.0 reshape.466
  243.7 2.9 copy.24
  246.6 4.0 reshape.466
  263.4 2.9 copy.24
  266.4 4.0 reshape.466
  283.2 2.9 copy.24
  286.1 4.0 reshape.466
  303.0 2.9 copy.24
  305.9 4.0 reshape.466
  322.8 2.9 copy.24
  325.7 4.0 reshape.466
  345.5 4.0 reshape.466
  362.3 2.9 copy.24
  365.2 4.0 reshape.466
  382.1 2.9 copy.24
  385.0 4.0 reshape.466
  404.8 4.0 reshape.466
  424.6 4.0 reshape.466
  441.4 2.9 copy.24
  444.4 4.0 reshape.466
  461.2 2.9 copy.24
  464.1 4.0 reshape.466
  481.0 2.9 copy.24
  483.9 4.0 reshape.466
  495.3 4.7 bitcast_multiply_fusion.4
  (287 shorter events, 217.6 us)
Async XLA Ops:
  6.5 172.4 %all-gather.2.cloned.1.call-start = ((), (), s32[]{:S(2)}) async-start(), calls=%async_computation | async-start | bytes 16908288 | tf_op jit(solution)/shard_map/all_gather | solution.py:98
  191.3 1.6 copy-start
  211.1 1.6 copy-start
  230.8 1.6 copy-start
  250.6 1.6 copy-start
  270.4 1.6 copy-start
  290.2 1.6 copy-start
  310.0 1.6 copy-start
  329.7 1.6 copy-start
  349.5 1.6 copy-start
  369.3 1.6 copy-start
  389.1 1.6 copy-start
  408.8 1.6 copy-start
  428.6 1.6 copy-start
  448.4 1.6 copy-start
  468.2 1.6 copy-start
  488.0 1.6 copy-start
Sparse Core Ops, SparseCore 0:
  10.0 168.9 all-gather.1
where the time goes:
time: 508 us; the launch traced here: 507 us
  waiting for transfers between devices  168 us (33%)
  local copies, waits for them, and re-layouts  168 us (33%)
  other arithmetic  89.5 us (18%)
  matrix products  66.9 us (13%)
  between operations  14.1 us (3%)
    all_gather x1, waiting for transfers between devices, per_device(): piece = lax.all_gather(spectra, 'row', axis=0, tiled=True)  167 us
    reshape x16, local copies, waits for them, and re-layouts, pair_block(): jnp.stack([real_part, imag_part], axis=2)  64.5 us
    another operation x16, local copies, waits for them, and re-layouts, pair_block(): jnp.stack([real_part, imag_part], axis=2)  47 us
    dot_general x16, matrix products, pair_block(): jnp.einsum('uv,pvk->puk', section_one, cross, precision=lax.Precision.HIGH)  34.5 us
    dot_general x16, matrix products, pair_block(): jnp.einsum('tck,pcuk->ptu', section_two, turned, precision=lax.Precision....  32.4 us
    dynamic_slice x16, local copies, waits for them, and re-layouts, correlate(): results = lax.map(one_group, (pieces, sign_pieces))  31.2 us
    slice x16, other arithmetic, pair_block(): return (2.0 * summed - real_part[:, :, :1]) * (1.0 / math.sqrt(8.0 * freq))  24 us
    slice x32, local copies, waits for them, and re-layouts, pair_block(): return (2.0 * summed - real_part[:, :, :1]) * (1.0 / math.sqrt(8.0 * freq))  17.6 us
  transfers between devices with their start and end apart: 1, of which 1 were waited for; matrix products, arithmetic and copies ran while one was open for 1% of the time, Pallas kernels for 0%

commit v1 on v0

--- a/solution.py
+++ b/solution.py
@@ -95,7 +95,9 @@
     weight = (
         pair_mask.astype(jnp.float32) * own_flags[:, None] * available.astype(jnp.float32)[None, :]
     )
-    piece = lax.all_gather(spectra, "row", axis=0, tiled=True)
+    piece = jnp.concatenate(
+        lax.all_to_all(jnp.stack([spectra] * lax.axis_size("row")), "row", 0, 0), axis=0
+    )
     corr = correlate(spectra, piece, jnp.ones((count, piece.shape[0]), jnp.float32), tables)
     return corr * weight[:, :, None]
 

time: 508 us -> 1110 us (2.19)
  waiting for transfers between devices: 168 us -> 719 us
  starting transfers between devices: 0.01 us -> 31.2 us
  matrix products: 66.9 us -> 92.3 us
  between operations: 14.1 us -> 0.77 us
    all_to_all x0 -> x1, waiting for transfers between devices: none -> 719 us  [per_device(): lax.all_to_all(jnp.stack([spectra] * lax.axis_size('row')), 'row', 0, 0)]
    all_gather x1 -> x0, waiting for transfers between devices: 167 us -> none  [per_device(): piece = lax.all_gather(spectra, 'row', axis=0, tiled=True)]
    all_to_all x0 -> x1, starting transfers between devices: none -> 31.2 us  [per_device(): lax.all_to_all(jnp.stack([spectra] * lax.axis_size('row')), 'row', 0, 0)]
    dot_general x16, matrix products: 34.5 us -> 59.9 us  [pair_block(): jnp.einsum('uv,pvk->puk', section_one, cross, precision=lax.Precision.HIGH)]
    another operation x0 -> x1, local copies, waits for them, and re-layouts: none -> 11.2 us  [per_device(): jnp.stack([spectra] * lax.axis_size('row'))]
  transfers between devices with their start and end apart: 1 -> 1, of which waited for: 1 -> 1; matrix products, arithmetic and copies ran while one was open for 1% -> 0% of each run, Pallas kernels for 0% -> 0%
where the time goes in v1:
time: 1110 us
  waiting for transfers between devices  719 us (65%)
  local copies, waits for them, and re-layouts  178 us (16%)
  matrix products  92.3 us (8%)
  other arithmetic  84.3 us (8%)
  starting transfers between devices  31.2 us (3%)
    all_to_all x1, waiting for transfers between devices, per_device(): lax.all_to_all(jnp.stack([spectra] * lax.axis_size('row')), 'row', 0, 0)  719 us
    reshape x16, local copies, waits for them, and re-layouts, pair_block(): jnp.stack([real_part, imag_part], axis=2)  64.9 us
    dot_general x16, matrix products, pair_block(): jnp.einsum('uv,pvk->puk', section_one, cross, precision=lax.Precision.HIGH)  59.9 us
    another operation x16, local copies, waits for them, and re-layouts, pair_block(): jnp.stack([real_part, imag_part], axis=2)  47 us
    dot_general x16, matrix products, pair_block(): jnp.einsum('tck,pcuk->ptu', section_two, turned, precision=lax.Precision....  32.4 us
    all_to_all x1, starting transfers between devices, per_device(): lax.all_to_all(jnp.stack([spectra] * lax.axis_size('row')), 'row', 0, 0)  31.2 us
    dynamic_slice x16, local copies, waits for them, and re-layouts, correlate(): results = lax.map(one_group, (pieces, sign_pieces))  31.1 us
  transfers between devices with their start and end apart: 1, of which 1 were waited for; matrix products, arithmetic and copies ran while one was open for 0% of the time, Pallas kernels for 0%

profile of v1, /device:TPU:33, one launch (start us, length us, event | category | flops | bytes accessed | tf_op | source)
XLA Modules:
  0.0 1107.1 jit_solution(1498292546320732834)
XLA Ops:
  0.0 11.2 %stack.8 = bf16[128,1,2,32768]{3,2,1,0:T(2,128)(2,1)} broadcast(bf16[2,32768]{1,0:T(2,128)(2,1)} %bitcast.84), dimensions={2,3} | broadcast | bytes 16908288 | tf_op jit(solution)/shard_map/stack | solution.py:99
  11.3 31.2 %all-to-all-start = ((bf16[128,1,2,32768]{3,2,1,0:T(2,128)(2,1)}), bf16[128,1,2,32768]{3,2,1,0:T(2,128)(2,1)}, u32[]{:S(2)}, u32[]{:S(2)}) async-start(bf16[128,1,2,32768]{3,2,1,0:T(2,128)(2,1)} %stack.8), calls=%async_computation | async-start | bytes 33554432 | tf_op jit(solution)/shard_map/all_to_all | solution.py:99
  45.1 718.9 %all-to-all-done = bf16[128,1,2,32768]{3,2,1,0:T(2,128)(2,1)} async-done(((bf16[128,1,2,32768]{3,2,1,0:T(2,128)(2,1)}), bf16[128,1,2,32768]{3,2,1,0:T(2,128)(2,1)}, u32[]{:S(2)}, u32[]{:S(2)}) %all-to-all-start) | async-done | bytes 16777248 | tf_op jit(solution)/shard_map/all_to_all | solution.py:99
  764.0 338.5 %while.13 = (s32[]{:T(128)}, f32[16,1,8,8192]{3,2,1,0:T(8,128)}, f32[1,2,32768]{2,1,0:T(2,128)S(1)}, bf16[16,8,2,32768]{3,2,1,0:T(2,128)(2,1)}, f32[256,128]{1,0...) while((s32[]{:T(128)}, f32[16,1,8,8192]{3,2,1,0:T(8,128)}, ...), condition=%wide.region_1.2_spmd.clone.clone.clone, body=%wide.region_0.1_spmd.clone.clone.clone.sunk | while | flops 1215889408 | bytes 48628976 | solution.py:85
  770.1 4.1 reshape.465
  791.3 4.1 reshape.465
  812.4 4.1 reshape.465
  816.5 3.7 fusion.71
  833.6 4.1 reshape.465
  854.8 4.1 reshape.465
  858.8 3.7 fusion.71
  875.9 4.1 reshape.465
  880.0 3.7 fusion.71
  897.1 4.1 reshape.465
  901.1 3.7 fusion.71
  918.2 4.1 reshape.465
  922.3 3.7 fusion.71
  939.4 4.1 reshape.465
  943.4 3.7 fusion.71
  960.5 4.1 reshape.465
  964.6 3.7 fusion.71
  981.7 4.1 reshape.465
  985.7 3.7 fusion.71
  1002.8 4.1 reshape.465
  1006.9 3.7 fusion.71
  1023.9 4.1 reshape.465
  1045.1 4.1 reshape.465
  1049.2 3.7 fusion.71
  1066.3 4.1 reshape.465
  1070.3 3.7 fusion.71
  1087.4 4.1 reshape.465
  1102.5 4.7 bitcast_multiply_fusion.4
  (261 shorter events, 233.1 us)
Async XLA Ops:
  11.2 31.3 %copy-start = (bf16[1,2,32768]{2,1,0:T(2,128)(2,1)S(1)}, bf16[1,2,32768]{2,1,0:T(2,128)(2,1)}, u32[]{:S(2)}) copy-start(bf16[1,2,32768]{2,1,0:T(2,128)(2,1)} %param.5) | copy-start | bytes 393220
  11.2 31.4 %copy-start.1 = (s32[128]{0:T(128)S(1)}, s32[128]{0:T(128)}, u32[]{:S(2)}) copy-start(s32[128]{0:T(128)} %param.7) | copy-start | bytes 1540
  11.3 33.9 %copy-start.2 = (s32[1,128]{1,0:T(1,128)S(1)}, s32[1,128]{1,0:T(1,128)}, u32[]{:S(2)}) copy-start(s32[1,128]{1,0:T(1,128)} %param.6) | copy-start | bytes 1540
  11.3 752.8 %all-to-all-start = ((bf16[128,1,2,32768]{3,2,1,0:T(2,128)(2,1)}), bf16[128,1,2,32768]{3,2,1,0:T(2,128)(2,1)}, u32[]{:S(2)}, u32[]{:S(2)}) async-start(bf16[128,1,2,32768]{3,2,1,0:T(2,128)(2,1)} %stack.8), calls=%async_computation | async-start | bytes 33554432 | tf_op jit(solution)/shard_map/all_to_all | solution.py:99
